TPU v7x, 256 devices: a whole 4x4x8 slice. The times are simulated.
256 devices in a mesh: blk: 16 (over x, z_hi), slab: 16 (over z_lo, y, core).
Axes of the slice: x: 4, y: 4, z: 8 (z_hi: 4, z_lo: 2; z = z_hi * 2 + z_lo), core: 2. Of those that a mesh axis runs over, the one named last changes fastest.
Arguments:
- zeta_sets: bfloat16 [16, 16384, 2048], P('blk', 'slab'), may hold values from -6 to 6
- coef_blocks: bfloat16 [64, 2, 2048, 256], P('blk', None, 'slab'), may hold values from -0.09375 to 0.09375
- pair_table: int32 [64, 2], P('blk'), may hold values from 0 to 1, each once within a row
- band_counts: int32 [64], P('blk'), may hold values from 64 to 256
- orbitals: bfloat16 [64, 16384, 256], P('blk', 'slab'), may hold values from -0.046875 to 0.046875
Outputs:
- exchange_field: float32 [64, 16384, 256], P('blk', 'slab')
- intersection: float32 [64, 256, 256], P('blk')
Inputs may be any that keep to these rules, and one draw needn't show every extreme that they name: Each row of pair_table names every number from 0 to 1 once.
All inputs are finite; a program needn't handle non-finite values.
Results may differ from a plain program's by a relative error of at most 0.0003.
Values may be sent and summed in bfloat16 or wider, within the bound.
A program may use at most 64 MiB of HBM per device.

v0:
```python
import jax
import jax.numpy as jnp
from jax import lax
from jax.sharding import PartitionSpec as P


def shifted(block, axis, distance):
    devices = range(lax.axis_size(axis))
    route = [((i - distance) % len(devices), i) for i in devices]
    return lax.ppermute(block, axis, route)


def cut_along(value, dim, length):
    before, after = (value.shape[:dim], value.shape[dim + 1 :])
    return jnp.moveaxis(value.reshape(*before, length, -1, *after), dim, 0)


def sent_and_summed(value, axis, dim):
    blocks = cut_along(value, dim, lax.axis_size(axis))
    arrived = lax.all_to_all(blocks, axis, split_axis=0, concat_axis=0, tiled=True)
    return arrived.sum(axis=0)


def rows_for(lines, length):
    spare = -lines.shape[0] % length
    if not spare:
        return lines
    return jnp.concatenate([lines, jnp.zeros((spare, *lines.shape[1:]), lines.dtype)])


def sent_to_all(value, axis):
    length = lax.axis_size(axis)
    return lax.all_to_all(
        jnp.broadcast_to(value[None], (length, *value.shape)), axis, 0, 0, tiled=True
    )


def joined_along(blocks, dim):
    blocks = jnp.moveaxis(blocks, 0, dim)
    dims = blocks.shape
    return blocks.reshape(*dims[:dim], dims[dim] * dims[dim + 1], *dims[dim + 2 :])


def collect(value, axis, dim):
    blocks = sent_to_all(value, axis)
    return joined_along(blocks, dim)


def total_of(value, axes):
    lines = value.reshape(-1, value.shape[-1])
    own = sent_and_summed(rows_for(lines, lax.axis_size(axes)), axes, 0)
    whole = collect(own, axes, 0)
    return whole[: len(lines)].reshape(value.shape)


def contract_padded(zeta_rows, coef_rows):
    return jnp.einsum("scr,ksrb->kcb", zeta_rows, coef_rows, preferred_element_type=jnp.float32)


def contract(zeta_rows, coef_rows):
    return contract_padded(zeta_rows, coef_rows)


def on_device(zeta_sets, coef_blocks, pair_table, band_counts, orbitals):
    inverse = jnp.argsort(pair_table, axis=1)
    ordered = jnp.take_along_axis(coef_blocks, inverse[:, :, None, None], axis=1)
    columns = jnp.arange(coef_blocks.shape[3], dtype=jnp.int32)
    keep = columns[None, :] < band_counts[:, None]
    ordered = jnp.where(keep[:, None, None, :], ordered, jnp.zeros((), jnp.bfloat16))
    previous = shifted(zeta_sets, "blk", 1)
    window_sets = jnp.concatenate([zeta_sets, previous], axis=0)
    fields = contract(window_sets, lax.all_gather(ordered, "slab", axis=2, tiled=True))
    masked = jnp.where(keep[:, None, :], orbitals.astype(jnp.float32), jnp.zeros((), jnp.float32))
    partial_value = jnp.einsum("kca,kcb->kab", masked, fields, precision=lax.Precision.HIGHEST)
    intersection = total_of(partial_value, "slab")
    return (fields, intersection)


def solution(mesh):
    return jax.shard_map(
        on_device,
        mesh=mesh,
        in_specs=(
            P("blk", "slab", None),
            P("blk", None, "slab", None),
            P("blk", None),
            P("blk"),
            P("blk", "slab", None),
        ),
        out_specs=(P("blk", "slab", None), P("blk", None, None)),
        check_vma=False,
    )
```

profile of v0, /device:TPU:1, one launch (start us, length us, event | category | flops | bytes accessed | tf_op | source)
XLA Modules:
  0.0 311.5 jit_solution(9005712388860684441)
XLA Ops:
  7.2 0.0 copy-start
  7.2 0.0 all-gather.2.cloned.1.call-start
  7.2 1.3 sort.17
  8.6 0.7 iota_compare_fusion
  9.3 0.1 copy.12
  9.4 0.1 copy.13
  9.5 0.1 reshape.58
  9.6 0.0 copy-done
  9.6 0.6 gather_fusion
  10.2 0.3 copy.14
  10.4 1.0 select_select_fusion
  11.5 0.0 all-gather.2.cloned.1.call-update
  11.5 0.0 copy-start.2
  11.5 3.9 %collective-permute-start = (bf16[1,1024,2048]{2,1,0:T(8,128)(2,1)}, bf16[1,1024,2048]{2,1,0:T(8,128)(2,1)}, u32[]{:S(2)}, u32[]{:S(2)}) collective-permute-start(bf16[1,1024,2048]{2,1,0:T(8,128)(2,1)} %param.5), channel_id=1, source_target_pairs={{240,0},{0,16},{16,32},{32,48},{48,64},{64,80},{80,96},{96,112},{1... | collective-permute-start | bytes 12582920 | tf_op jit(solution)/shard_map/ppermute | solution.py:10
  15.4 225.1 %collective-permute-done = bf16[1,1024,2048]{2,1,0:T(8,128)(2,1)} collective-permute-done((bf16[1,1024,2048]{2,1,0:T(8,128)(2,1)}, bf16[1,1024,2048]{2,1,0:T(8,128)(2,1)}, u32[]{:S(2)}, u32[]{:S(2)}) %collective-permute-start) | collective-permute-done | bytes 4194336 | tf_op jit(solution)/shard_map/ppermute | solution.py:10
  240.5 0.0 all-gather.2.cloned.1.call-done
  240.5 13.7 %fusion = f32[4,256,1024,1]{2,1,3,0:T(8,128)S(1)} fusion(bf16[4,2,2048,256]{2,3,1,0:T(8,128)(2,1)} %all-gather.2.cloned.1.call-done, bf16[1,1024,2048]{2,1,0:T(8,128)(2,1)} %collective-permute-done, bf16[1,1024,2048]{2,1,0:T(8,128)(2,1)} %param.5), kind=kOutput, calls=%fused_computation.2 | convolution fusion | flops 8594128896 | bytes 20971520 | tf_op jit(solution)/shard_map/scr,ksrb->kcb/dot_general | solution.py:57
  254.2 0.0 copy-start.1
  254.2 1.9 copy-done.1
  256.1 0.0 copy-done.2
  256.1 5.3 %fusion.3 = f32[4,256,256]{2,1,0:T(8,128)S(1)} fusion(f32[4,256,1024,1]{2,1,3,0:T(8,128)S(1)} %fusion, bf16[4,1024,256]{2,1,0:T(8,128)(2,1)S(1)} %copy-done.2, pred[4,256]{1,0:T(4,128)(4,1)S(1)} %iota_compare_fusion), kind=kOutput, calls=%fused_computation.5 | convolution fusion | flops 3223322624 | bytes 7341056 | tf_op jit(solution)/shard_map/kca,kcb->kab/dot_general | solution.py:74
  261.5 20.6 %all_to_all.10 = f32[16,64,256]{2,1,0:T(8,128)S(1)} all-to-all(f32[16,64,256]{2,1,0:T(8,128)S(1)} %bitcast.19), channel_id=1, replica_groups=mesh['blk'=16,'slab'=16] {'slab'}, dimensions={0} | all-to-all | bytes 2097152 | tf_op jit(solution)/shard_map/all_to_all | solution.py:20
  282.1 0.1 reduce_sum.9
  282.2 1.1 broadcast_in_dim.49
  283.2 4.7 %all-to-all-start.1 = ((f32[16,64,256]{2,1,0:T(8,128)}), f32[16,64,256]{2,1,0:T(8,128)S(1)}, u32[]{:S(2)}, u32[]{:S(2)}) async-start(f32[16,64,256]{2,1,0:T(8,128)} %broadcast_in_dim.49), calls=%async_computation.1 | async-start | bytes 2097152 | tf_op jit(solution)/shard_map/all_to_all | solution.py:33
  288.0 5.4 %copy.16 = f32[4,1024,256]{2,1,0:T(8,128)} copy(f32[4,1024,256]{1,2,0:T(8,128)} %bitcast.17) | data formatting | bytes 8388608
  293.3 10.4 %all-to-all-done.1 = f32[16,64,256]{2,1,0:T(8,128)S(1)} async-done(((f32[16,64,256]{2,1,0:T(8,128)}), f32[16,64,256]{2,1,0:T(8,128)S(1)}, u32[]{:S(2)}, u32[]{:S(2)}) %all-to-all-start.1) | async-done | bytes 1048608 | tf_op jit(solution)/shard_map/all_to_all | solution.py:33
  303.7 1.0 copy.20
  (3 shorter events, 0.0 us)
Async XLA Ops:
  7.2 2.4 copy-start
  7.2 233.3 %all-gather.2.cloned.1.call-start = ((), (), s32[]{:S(2)}) async-start(), calls=%async_computation.2 | async-start | bytes 8912896 | tf_op jit(solution)/shard_map/all_gather | solution.py:72
  11.5 244.6 %copy-start.2 = (bf16[4,1024,256]{2,1,0:T(8,128)(2,1)S(1)}, bf16[4,1024,256]{2,1,0:T(8,128)(2,1)}, u32[]{:S(2)}) copy-start(bf16[4,1024,256]{2,1,0:T(8,128)(2,1)} %param.9) | copy-start | bytes 6291460
  11.5 229.0 %collective-permute-start = (bf16[1,1024,2048]{2,1,0:T(8,128)(2,1)}, bf16[1,1024,2048]{2,1,0:T(8,128)(2,1)}, u32[]{:S(2)}, u32[]{:S(2)}) collective-permute-start(bf16[1,1024,2048]{2,1,0:T(8,128)(2,1)} %param.5), channel_id=1, source_target_pairs={{240,0},{0,16},{16,32},{32,48},{48,64},{64,80},{80,96},{96,112},{1... | collective-permute-start | bytes 12582920 | tf_op jit(solution)/shard_map/ppermute | solution.py:10
  254.2 1.9 copy-start.1
  283.2 20.5 %all-to-all-start.1 = ((f32[16,64,256]{2,1,0:T(8,128)}), f32[16,64,256]{2,1,0:T(8,128)S(1)}, u32[]{:S(2)}, u32[]{:S(2)}) async-start(f32[16,64,256]{2,1,0:T(8,128)} %broadcast_in_dim.49), calls=%async_computation.1 | async-start | bytes 2097152 | tf_op jit(solution)/shard_map/all_to_all | solution.py:33
Sparse Core Ops, SparseCore 0:
  11.6 181.5 all-gather.1
where the time goes:
time: 312 us
  waiting for transfers between devices  235 us (75%)
  blocking collectives  20.6 us (7%)
  matrix products  19.1 us (6%)
  between operations  14.1 us (5%)
  local copies, waits for them, and re-layouts  10.5 us (3%)
  starting transfers between devices  8.63 us (3%)
  other arithmetic  3.13 us (1%)
    ppermute x1, waiting for transfers between devices, shifted(): return lax.ppermute(block, axis, route)  225 us
    all_to_all x1, blocking collectives, sent_and_summed(): lax.all_to_all(blocks, axis, split_axis=0, concat_axis=0, tiled=True)  20.6 us
    dot_general x1, matrix products, contract_padded(): jnp.einsum('scr,ksrb->kcb', zeta_rows, coef_rows, preferred_element_type=...  13.7 us
    all_to_all x1, waiting for transfers between devices, sent_to_all(): lax.all_to_all(jnp.broadcast_to(value[None], (length, *value.shape)), axi...  10.4 us
    unnamed x8, local copies, waits for them, and re-layouts  8.27 us
  transfers between devices with their start and end apart: 3, of which 2 were waited for; matrix products, arithmetic and copies ran while one was open for 2% of the time, Pallas kernels for 0%

commit v1 on v0

v1 whole, which is shorter than its diff:
```python
import functools

import jax
import jax.numpy as jnp
from jax import lax
from jax.experimental import pallas as pl
from jax.experimental.pallas import tpu as pltpu
from jax.sharding import PartitionSpec as P

NZ, NY, NC = 2, 4, 2
LEVELS = 32767.0
TILE = 256


def slab_at(z, y, c):
    return (z * NY + y) * NC + c


def kernel(
    zeta_in, coef_in, orb_in, field_out, inter_out,
    zeta, coef, orb, psend, precv, ssend, srecv, field,
    part, rsib, half, ry, quarter, rz, final,
    load_sem, pair_sem, pair_out, cz_sem, ag_sem, ag_out, p_sem, p_out, ar_sem, ar_out, store_sem,
):
    kpts = orb.shape[0]
    rows = zeta.shape[0]
    tile = min(TILE, rows)
    tiles = rows // tile
    blk, slab = lax.axis_index("blk"), lax.axis_index("slab")
    nblk = lax.axis_size("blk")
    c = lax.rem(slab, NC)
    y = lax.rem(slab // NC, NY)
    z = slab // (NC * NY)
    after, before = lax.rem(blk + 1, nblk), lax.rem(blk + nblk - 1, nblk)
    ys = [lax.rem(y + d, NY) for d in range(NY)]
    at_y = [{"slab": slab_at(z, ys[d], c)} for d in range(NY)]
    at_z = {"slab": slab_at(1 - z, y, c)}
    at_c = {"slab": slab_at(z, y, 1 - c)}
    at_after = {"blk": after, "slab": slab}

    def near(other, zz):
        return {"blk": other, "slab": slab_at(zz, y, c)}

    def send(src, dst, out, arrived, where):
        copy = pltpu.make_async_remote_copy(
            src_ref=src, dst_ref=dst, send_sem=out, recv_sem=arrived,
            device_id=where, device_id_type=pl.DeviceIdType.MESH,
        )
        copy.start()
        return copy

    def landed(ref, sem):
        pltpu.make_async_copy(ref, ref, sem).wait()

    barrier = pltpu.get_barrier_semaphore()
    greeted = [near(before, 0), near(before, 1), near(after, 0), near(after, 1), at_y[1], at_y[2], at_y[3], at_z, at_c]
    for where in greeted:
        pl.semaphore_signal(barrier, inc=1, device_id=where, device_id_type=pl.DeviceIdType.MESH)
    pl.semaphore_wait(barrier, len(greeted))

    sent = []
    for k in range(kpts):
        for zz in range(NZ):
            sent.append(send(coef_in.at[k], coef.at[k, z, y, c], pair_out.at[k, zz], pair_sem.at[k, z], near(before, zz)))
    own = pltpu.make_async_copy(coef_in.at[pl.ds(kpts, kpts)], coef.at[pl.ds(kpts, kpts), z, y, c], load_sem.at[0])
    own.start()
    sent.append(send(coef_in.at[pl.ds(kpts, kpts)], coef.at[pl.ds(kpts, kpts), z, y, c], cz_sem.at[1], cz_sem.at[0], at_z))
    load_zeta = pltpu.make_async_copy(zeta_in, zeta, load_sem.at[1])
    load_zeta.start()
    load_orb = pltpu.make_async_copy(orb_in, orb, load_sem.at[2])
    load_orb.start()

    def pair(ch, at):
        return coef.at[ch, :, at, c]

    def spread(ch):
        for n, where in enumerate((at_y[1], at_y[3], at_c)):
            sent.append(send(pair(ch, y), pair(ch, y), ag_out.at[ch, n], ag_sem.at[ch, n], where))

    def relay(ch):
        landed(pair(ch, ys[3]), ag_sem.at[ch, 0])
        one = coef.at[ch, 0, ys[3], c]
        sent.append(send(one, one, ag_out.at[ch, 3], ag_sem.at[ch, 3], at_y[1]))
        sent.append(send(pair(ch, ys[3]), pair(ch, ys[3]), ag_out.at[ch, 5], ag_sem.at[ch, 5], at_c))
        landed(pair(ch, ys[1]), ag_sem.at[ch, 1])
        one = coef.at[ch, 1, ys[1], c]
        sent.append(send(one, one, ag_out.at[ch, 4], ag_sem.at[ch, 4], at_y[3]))
        sent.append(send(pair(ch, ys[1]), pair(ch, ys[1]), ag_out.at[ch, 6], ag_sem.at[ch, 6], at_c))

    def far(ch):
        landed(coef.at[ch, 0, ys[2], c], ag_sem.at[ch, 3])
        landed(coef.at[ch, 1, ys[2], c], ag_sem.at[ch, 4])
        sent.append(send(pair(ch, ys[2]), pair(ch, ys[2]), ag_out.at[ch, 7], ag_sem.at[ch, 7], at_c))

    def joined(ch):
        for n, at in ((2, y), (5, ys[3]), (6, ys[1]), (7, ys[2])):
            landed(coef.at[ch, :, at, 1 - c], ag_sem.at[ch, n])

    def gather(chunks, first):
        for ch in chunks:
            first(ch)
            spread(ch)
        for ch in chunks:
            relay(ch)
        for ch in chunks:
            far(ch)
        for ch in chunks:
            joined(ch)

    def moved(ch):
        landed(coef.at[ch, 0, y, c], pair_sem.at[ch, 0])
        landed(coef.at[ch, 1, y, c], pair_sem.at[ch, 1])

    def product(ch, r):
        lines = zeta[pl.ds(pl.multiple_of(r * tile, tile), tile), :]
        return jnp.dot(lines, coef[ch].reshape(zeta.shape[1], -1), preferred_element_type=jnp.float32)

    def term(k):
        def step(r, carry):
            value = product(k, r)
            top = jnp.maximum(jnp.max(jnp.abs(value), axis=0, keepdims=True), 1e-30)
            level = jnp.round(value * (LEVELS / top)).astype(jnp.int32)
            psend[k, pl.ds(pl.multiple_of(r * tile, tile), tile), :] = level.astype(jnp.int16)
            ssend[k, r] = top / LEVELS
            return carry

        lax.fori_loop(0, tiles, step, 0)
        sent.append(send(psend.at[k], precv.at[k], p_out.at[k, 0], p_sem.at[k, 0], at_after))
        sent.append(send(ssend.at[k], srecv.at[k], p_out.at[k, 1], p_sem.at[k, 1], at_after))

    def own_term(k):
        def step(r, carry):
            field[k, pl.ds(pl.multiple_of(r * tile, tile), tile), :] = product(kpts + k, r)
            return carry

        lax.fori_loop(0, tiles, step, 0)

    stores = []

    def combine(k):
        landed(precv.at[k], p_sem.at[k, 0])
        landed(srecv.at[k], p_sem.at[k, 1])

        def step(r, carry):
            at = pl.ds(pl.multiple_of(r * tile, tile), tile)
            value = field[k, at, :] + precv[k, at, :].astype(jnp.int32).astype(jnp.float32) * srecv[k, r]
            field[k, at, :] = value
            high = value.astype(jnp.bfloat16)
            low = (value - high.astype(jnp.float32)).astype(jnp.bfloat16)
            lines = orb[k, at, :]
            over = (((0,), (0,)), ((), ()))
            added = lax.dot_general(lines, high, over, preferred_element_type=jnp.float32)
            added += lax.dot_general(lines, low, over, preferred_element_type=jnp.float32)
            added = added.reshape(part.shape[1:])

            @pl.when(r == 0)
            def _():
                part[k] = added

            @pl.when(r > 0)
            def _():
                part[k] += added

            return carry

        lax.fori_loop(0, tiles, step, 0)
        out = pltpu.make_async_copy(field.at[k], field_out.at[k], store_sem.at[0, k])
        out.start()
        stores.append(out)

    def reduce(k):
        sent.append(send(part.at[k, 1 - c], rsib.at[k], ar_out.at[k, 0], ar_sem.at[k, 0], at_c))
        landed(rsib.at[k], ar_sem.at[k, 0])
        half[k] = part[k, c] + rsib[k]
        for d in range(1, NY):
            sent.append(send(half.at[k, ys[d]], ry.at[k, d - 1], ar_out.at[k, d], ar_sem.at[k, d], at_y[d]))
        total = half[k, y]
        for d in range(1, NY):
            landed(ry.at[k, d - 1], ar_sem.at[k, d])
            total = total + ry[k, d - 1]
        quarter[k] = total
        sent.append(send(quarter.at[k], rz.at[k], ar_out.at[k, 4], ar_sem.at[k, 4], at_z))
        landed(rz.at[k], ar_sem.at[k, 4])
        final[k, c, y] = quarter[k] + rz[k]
        for d in range(1, NY):
            sent.append(send(final.at[k, c, y], final.at[k, c, y], ar_out.at[k, 4 + d], ar_sem.at[k, 4 + d], at_y[d]))
        for d in range(1, NY):
            landed(final.at[k, c, ys[NY - d]], ar_sem.at[k, 4 + d])
        sent.append(send(final.at[k, c], final.at[k, c], ar_out.at[k, 8], ar_sem.at[k, 8], at_c))
        landed(final.at[k, 1 - c], ar_sem.at[k, 8])
        out = pltpu.make_async_copy(final.at[k], inter_out.at[k], store_sem.at[1, k])
        out.start()
        stores.append(out)

    gather((0,), moved)
    load_zeta.wait()
    term(0)
    gather((1,), moved)
    term(1)
    gather((2, 3), moved)
    term(2)
    term(3)
    own.wait()
    landed(coef.at[pl.ds(kpts, kpts), 1 - z, y, c], cz_sem.at[0])
    gather((4, 5), lambda ch: None)
    own_term(0)
    own_term(1)
    load_orb.wait()
    combine(0)
    reduce(0)
    gather((6, 7), lambda ch: None)
    own_term(2)
    own_term(3)
    for k in range(1, kpts):
        combine(k)
        reduce(k)
    for copy in sent:
        copy.wait_send()
    for copy in stores:
        copy.wait()


def exchange(zeta, coefs, orbitals):
    rows, points = zeta.shape
    kpts, _, bands = orbitals.shape
    tile = min(TILE, rows)
    share = coefs.shape[1]
    slice_ = bands // (NC * NY)
    f32, bf16, i16 = jnp.float32, jnp.bfloat16, jnp.int16
    anywhere = pl.BlockSpec(memory_space=pltpu.HBM)
    dma = pltpu.SemaphoreType.DMA
    return pl.pallas_call(
        kernel,
        out_shape=(
            jax.ShapeDtypeStruct((kpts, rows, bands), f32),
            jax.ShapeDtypeStruct((kpts, NC, NY, slice_, bands), f32),
        ),
        in_specs=[anywhere] * 3,
        out_specs=(anywhere, anywhere),
        scratch_shapes=[
            pltpu.VMEM((rows, points), bf16),
            pltpu.VMEM((2 * kpts, NZ, NY, NC, share, bands), bf16),
            pltpu.VMEM((kpts, rows, bands), bf16),
            pltpu.VMEM((kpts, rows, bands), i16),
            pltpu.VMEM((kpts, rows, bands), i16),
            pltpu.VMEM((kpts, rows // tile, 1, bands), f32),
            pltpu.VMEM((kpts, rows // tile, 1, bands), f32),
            pltpu.VMEM((kpts, rows, bands), f32),
            pltpu.VMEM((kpts, NC, NY, slice_, bands), f32),
            pltpu.VMEM((kpts, NY, slice_, bands), f32),
            pltpu.VMEM((kpts, NY, slice_, bands), f32),
            pltpu.VMEM((kpts, NY - 1, slice_, bands), f32),
            pltpu.VMEM((kpts, slice_, bands), f32),
            pltpu.VMEM((kpts, slice_, bands), f32),
            pltpu.VMEM((kpts, NC, NY, slice_, bands), f32),
            dma((3,)),
            dma((kpts, NZ)),
            dma((kpts, NZ)),
            dma((2,)),
            dma((2 * kpts, 8)),
            dma((2 * kpts, 8)),
            dma((kpts, 2)),
            dma((kpts, 2)),
            dma((kpts, 9)),
            dma((kpts, 9)),
            dma((2, kpts)),
        ],
        compiler_params=pltpu.CompilerParams(collective_id=0, has_side_effects=True, vmem_limit_bytes=60 * 1024 * 1024),
        name="exchange",
    )(zeta, coefs, orbitals)


def on_device(zeta_sets, coef_blocks, pair_table, band_counts, orbitals):
    swap = (pair_table[:, :1] == 1)[:, :, None]
    columns = jnp.arange(coef_blocks.shape[3], dtype=jnp.int32)
    keep = columns[None, :] < band_counts[:, None]
    zero = jnp.zeros((), jnp.bfloat16)
    straight, crossed = coef_blocks[:, 0], coef_blocks[:, 1]
    nearest = jnp.where(keep[:, None, :], jnp.where(swap, crossed, straight), zero)
    previous = jnp.where(keep[:, None, :], jnp.where(swap, straight, crossed), zero)
    coefs = jnp.concatenate([previous, nearest], axis=0)
    fields, intersection = exchange(zeta_sets[0], coefs, orbitals)
    kpts, bands = keep.shape
    intersection = intersection.reshape(kpts, bands, bands)
    intersection = jnp.where(keep[:, :, None], intersection, jnp.zeros((), jnp.float32))
    return fields, intersection


def solution(mesh):
    return jax.shard_map(
        on_device,
        mesh=mesh,
        in_specs=(
            P("blk", "slab", None),
            P("blk", None, "slab", None),
            P("blk", None),
            P("blk"),
            P("blk", "slab", None),
        ),
        out_specs=(P("blk", "slab", None), P("blk", None, None)),
        check_vma=False,
    )
```

time: 312 us -> 199 us (0.64)
  waiting for transfers between devices: 235 us -> 0 us
  Pallas kernels: 0 us -> 188 us
  blocking collectives: 20.6 us -> 0 us
  matrix products: 19.1 us -> 0 us
  between operations: 14.1 us -> 0.64 us
  starting transfers between devices: 8.63 us -> 0 us
  local copies, waits for them, and re-layouts: 10.5 us -> 4.57 us
    ppermute x1 -> x0, waiting for transfers between devices: 225 us -> none  [shifted(): return lax.ppermute(block, axis, route)]
    pallas_call x0 -> x1, Pallas kernels: none -> 188 us  [exchange(): pl.pallas_call(kernel, out_shape=(jax.ShapeDtypeStruct((kpts, rows, bands...]
    all_to_all x1 -> x0, blocking collectives: 20.6 us -> none  [sent_and_summed(): lax.all_to_all(blocks, axis, split_axis=0, concat_axis=0, tiled=True)]
    dot_general x2 -> x0, matrix products: 19.1 us -> none  [the longest x1 13.7 us: contract_padded(): jnp.einsum('scr,ksrb->kcb', zeta_rows, coef_rows, preferred_element_type=...]
    all_to_all x1 -> x0, waiting for transfers between devices: 10.4 us -> none  [sent_to_all(): lax.all_to_all(jnp.broadcast_to(value[None], (length, *value.shape)), axi...]
    all_to_all x1 -> x0, starting transfers between devices: 4.71 us -> none  [sent_to_all(): lax.all_to_all(jnp.broadcast_to(value[None], (length, *value.shape)), axi...]
    ppermute x1 -> x0, starting transfers between devices: 3.89 us -> none  [shifted(): return lax.ppermute(block, axis, route)]
    unnamed x8 -> x1, local copies, waits for them, and re-layouts: 8.27 us -> 4.57 us
  transfers between devices with their start and end apart: 3 -> 0, of which waited for: 2 -> 0; matrix products, arithmetic and copies ran while one was open for 2% -> 0% of each run, Pallas kernels for 0% -> 0%
where the time goes in v1:
time: 199 us
  Pallas kernels  188 us (94%)
  other arithmetic  5.79 us (3%)
  local copies, waits for them, and re-layouts  4.57 us (2%)
    pallas_call x1, Pallas kernels, exchange(): pl.pallas_call(kernel, out_shape=(jax.ShapeDtypeStruct((kpts, rows, bands...  188 us
    unnamed x1, local copies, waits for them, and re-layouts  4.57 us

profile of v1, /device:TPU:1, one launch (start us, length us, event | category | flops | bytes accessed | tf_op | source)
XLA Modules:
  0.0 199.3 jit_solution(126514904428847534)
XLA Ops:
  0.6 0.7 iota_compare_fusion
  1.4 0.7 compare_bitcast_fusion
  2.0 1.1 fusion
  3.2 0.8 pad_maximum_fusion.coef_in
  4.0 188.3 %exchange.1 = (f32[4,1024,256]{2,1,0:T(8,128)}, f32[4,2,4,32,256]{4,3,2,1,0:T(8,128)}) custom-call(bf16[1024,2048]{1,0:T(8,128)(2,1)} %bitcast.19, bf16[8,128,256]{2,1,0:T(8,128)(2,1)} %pad_maximum_fusion.coef_in, bf16[4,1024,256]{2,1,0:T(8,128)(2,1)} %orb_in.1), custom_call_target="tpu_custom_call" | custom-call | tf_op jit(solution)/shard_map/exchange/pallas_call | solution.py:232
  192.3 2.4 %bitcast_select_fusion = f32[4,256,256]{2,1,0:T(8,128)} fusion(f32[4,2,4,32,256]{4,3,2,1,0:T(8,128)} %get-tuple-element.5, pred[4,256]{1,0:T(4,128)(4,1)S(1)} %iota_compare_fusion), kind=kLoop, calls=%fused_computation | loop fusion | flops 262144 | bytes 2098176 | tf_op jit(solution)/shard_map/jit(_where)/select_n | solution.py:285
  194.7 4.6 %copy.12 = f32[4,1024,256]{2,1,0:T(8,128)} copy(f32[4,1024,256]{2,1,0:T(8,128)} %get-tuple-element.10) | data formatting | bytes 8388608

commit v2 on v1

v2 whole, which is shorter than its diff:
```python
import functools

import jax
import jax.numpy as jnp
from jax import lax
from jax.experimental import pallas as pl
from jax.experimental.pallas import tpu as pltpu
from jax.sharding import PartitionSpec as P

NZ, NY, NC = 2, 4, 2
LEVELS = 32767.0
TILE = 256
SPLIT_Z = 4
RELAY = (0, 12, 11, 0)
RELAY_UNIT = 32


def slab_at(z, y, c):
    return (z * NY + y) * NC + c


def kernel(
    pair_table, counts, zeta_in, coef_in, orb_in, field, final,
    zeta, raw, picked, coef, orb, psend, precv, middle, ssend, srecv,
    part, rsib, half, ry, quarter, rz,
    load_sem, pair_sem, pair_out, cz_sem, ag_sem, ag_out, p_sem, p_out, relay_sem, relay_out, ar_sem, ar_out,
):
    kpts, rows, bands = field.shape
    tile = min(TILE, rows)
    tiles = rows // tile
    blk, slab = lax.axis_index("blk"), lax.axis_index("slab")
    nblk = lax.axis_size("blk")
    nx, nz = nblk // SPLIT_Z, NZ * SPLIT_Z
    c = lax.rem(slab, NC)
    y = lax.rem(slab // NC, NY)
    z = slab // (NC * NY)
    x = blk // SPLIT_Z
    height = lax.rem(blk, SPLIT_Z) * NZ + z
    after, before = lax.rem(blk + 1, nblk), lax.rem(blk + nblk - 1, nblk)
    ys = [lax.rem(y + d, NY) for d in range(NY)]
    at_y = [{"slab": slab_at(z, ys[d], c)} for d in range(NY)]
    at_z = {"slab": slab_at(1 - z, y, c)}
    at_c = {"slab": slab_at(z, y, 1 - c)}
    at_after = {"blk": after, "slab": slab}

    def near(other, zz):
        return {"blk": other, "slab": slab_at(zz, y, c)}

    def up(xx, level):
        level = lax.rem(level, nz)
        return {"blk": lax.rem(xx, nx) * SPLIT_Z + level // NZ, "slab": slab_at(lax.rem(level, NZ), y, c)}

    def crossing(level):
        return (lax.rem(level, nz) + NZ) // nz

    below, above = height + nz - 3, height + 3
    relay_to, relay_from = up(x, below), up(x, above)
    forward_to = up(x + crossing(above), below)
    forward_from = up(x + nx - crossing(height + nz - NZ), above)

    def send(src, dst, out, arrived, where):
        copy = pltpu.make_async_remote_copy(
            src_ref=src, dst_ref=dst, send_sem=out, recv_sem=arrived,
            device_id=where, device_id_type=pl.DeviceIdType.MESH,
        )
        copy.start()
        sent.append(copy)

    def landed(ref, sem):
        pltpu.make_async_copy(ref, ref, sem).wait()

    sent = []
    load_raw = pltpu.make_async_copy(coef_in, raw, load_sem.at[0])
    load_raw.start()
    load_zeta = pltpu.make_async_copy(zeta_in, zeta, load_sem.at[1])
    load_zeta.start()
    load_orb = pltpu.make_async_copy(orb_in, orb, load_sem.at[2])
    load_orb.start()
    barrier = pltpu.get_barrier_semaphore()
    greeted = [
        near(before, 0), near(before, 1), near(after, 0), near(after, 1), at_y[1], at_y[2], at_y[3], at_z, at_c,
        relay_to, relay_from, forward_to, forward_from,
    ]
    for where in greeted:
        pl.semaphore_signal(barrier, inc=1, device_id=where, device_id_type=pl.DeviceIdType.MESH)
    load_raw.wait()
    for k in range(kpts):
        swap = jnp.full(raw.shape[2:], pair_table[0, k], jnp.int32) == 1
        one, two = raw[k, 0], raw[k, 1]
        picked[k] = jnp.where(swap, one, two)
        near_set = jnp.where(swap, two, one)
        picked[kpts + k] = near_set
        coef[kpts + k, z, y, c] = near_set
    pl.semaphore_wait(barrier, len(greeted))

    wide, narrow = pl.ds(0, bands), bands // 2
    pieces = [(0, pl.ds(0, narrow)), (0, pl.ds(narrow, narrow))] + [(k, wide) for k in range(1, kpts)]
    for n, (k, cols) in enumerate(pieces):
        for zz in range(NZ):
            send(picked.at[k, :, cols], coef.at[k, z, y, c, :, cols], pair_out.at[n, zz], pair_sem.at[n, z], near(before, zz))
    nearest = pl.ds(kpts, kpts)
    send(picked.at[nearest], coef.at[nearest, z, y, c], cz_sem.at[1], cz_sem.at[0], at_z)

    def view(n, at, cc):
        if n == len(pieces):
            return coef.at[nearest, :, at, cc]
        return coef.at[pieces[n][0], :, at, cc, :, pieces[n][1]]

    def spread(n):
        for lane, where in enumerate((at_y[1], at_y[3], at_y[2], at_c)):
            send(view(n, y, c), view(n, y, c), ag_out.at[n, lane], ag_sem.at[n, lane], where)

    def pass_on(n):
        for lane, at in enumerate((ys[3], ys[1], ys[2])):
            landed(view(n, at, c), ag_sem.at[n, lane])
            send(view(n, at, c), view(n, at, c), ag_out.at[n, 4 + lane], ag_sem.at[n, 4 + lane], at_c)

    def joined(n):
        for lane, at in ((3, y), (4, ys[3]), (5, ys[1]), (6, ys[2])):
            landed(view(n, at, 1 - c), ag_sem.at[n, lane])

    def moved(n):
        k, cols = pieces[n]
        for zz in range(NZ):
            landed(coef.at[k, zz, y, c, :, cols], pair_sem.at[n, zz])

    def begin(n):
        if n == len(pieces):
            landed(coef.at[nearest, 1 - z, y, c], cz_sem.at[0])
        else:
            moved(n)
        spread(n)

    def product(ch, r, cols):
        lines = zeta[pl.ds(pl.multiple_of(r * tile, tile), tile), :]
        block = coef[ch, :, :, :, :, cols]
        return jnp.dot(lines, block.reshape(zeta.shape[1], block.shape[-1]), preferred_element_type=jnp.float32)

    def extra(k):
        return rows * RELAY[k] // RELAY_UNIT

    def parts(k):
        return pl.ds(0, rows - extra(k)), pl.ds(rows - extra(k), extra(k))

    def term(n):
        k, cols = pieces[n]

        def step(r, carry):
            value = product(k, r, cols)
            top = jnp.maximum(jnp.max(jnp.abs(value), axis=0, keepdims=True), 1e-30)
            level = jnp.round(value * (LEVELS / top)).astype(jnp.int32)
            psend[k, pl.ds(pl.multiple_of(r * tile, tile), tile), cols] = level.astype(jnp.int16)
            ssend[k, r, :, cols] = top / LEVELS
            return carry

        lax.fori_loop(0, tiles, step, 0)
        direct, other = parts(k)
        if extra(k):
            send(psend.at[k, other], middle.at[k, pl.ds(0, extra(k))], relay_out.at[k, 0], relay_sem.at[k, 0], relay_to)
        send(ssend.at[k, :, :, cols], srecv.at[k, :, :, cols], p_out.at[n, 1], p_sem.at[n, 1], at_after)
        send(psend.at[k, direct, cols], precv.at[k, direct, cols], p_out.at[n, 0], p_sem.at[n, 0], at_after)

    def forward(k):
        if extra(k):
            held = middle.at[k, pl.ds(0, extra(k))]
            landed(held, relay_sem.at[k, 0])
            send(held, precv.at[k, parts(k)[1]], relay_out.at[k, 1], relay_sem.at[k, 1], forward_to)

    def own_term(k):
        def step(r, carry):
            field[k, pl.ds(pl.multiple_of(r * tile, tile), tile), :] = product(kpts + k, r, wide)
            return carry

        lax.fori_loop(0, tiles, step, 0)

    def arrived(k):
        direct, other = parts(k)
        for n, (owner, cols) in enumerate(pieces):
            if owner == k:
                landed(precv.at[k, direct, cols], p_sem.at[n, 0])
                landed(srecv.at[k, :, :, cols], p_sem.at[n, 1])
        if extra(k):
            landed(precv.at[k, other], relay_sem.at[k, 1])

    def combine(k):
        keep = lax.broadcasted_iota(jnp.int32, (1, bands), 1) < counts[k]
        weight = jnp.where(keep, 1.0, 0.0)
        weight_low = weight.astype(jnp.bfloat16)

        def step(r, carry):
            at = pl.ds(pl.multiple_of(r * tile, tile), tile)
            value = field[k, at, :] + precv[k, at, :].astype(jnp.int32).astype(jnp.float32) * srecv[k, r]
            value = value * weight
            field[k, at, :] = value
            high = value.astype(jnp.bfloat16)
            low = (value - high.astype(jnp.float32)).astype(jnp.bfloat16)
            lines = orb[k, at, :] * weight_low
            over = (((0,), (0,)), ((), ()))
            added = lax.dot_general(lines, high, over, preferred_element_type=jnp.float32)
            added += lax.dot_general(lines, low, over, preferred_element_type=jnp.float32)
            added = added.reshape(part.shape[1:])

            @pl.when(r == 0)
            def _():
                part[k] = added

            @pl.when(r > 0)
            def _():
                part[k] += added

            return carry

        lax.fori_loop(0, tiles, step, 0)
        send(part.at[k, 1 - c], rsib.at[k], ar_out.at[k, 0], ar_sem.at[k, 0], at_c)

    def scatter_y(k):
        landed(rsib.at[k], ar_sem.at[k, 0])
        half[k] = part[k, c] + rsib[k]
        for d in range(1, NY):
            send(half.at[k, ys[d]], ry.at[k, d - 1], ar_out.at[k, d], ar_sem.at[k, d], at_y[d])

    def swap_z(k):
        total = half[k, y]
        for d in range(1, NY):
            landed(ry.at[k, d - 1], ar_sem.at[k, d])
            total = total + ry[k, d - 1]
        quarter[k] = total
        send(quarter.at[k], rz.at[k], ar_out.at[k, 4], ar_sem.at[k, 4], at_z)

    def gather_y(k):
        landed(rz.at[k], ar_sem.at[k, 4])
        final[k, c, y] = quarter[k] + rz[k]
        for d in range(1, NY):
            send(final.at[k, c, y], final.at[k, c, y], ar_out.at[k, 4 + d], ar_sem.at[k, 4 + d], at_y[d])

    def gather_c(k):
        for d in range(1, NY):
            landed(final.at[k, c, ys[NY - d]], ar_sem.at[k, 4 + d])
        send(final.at[k, c], final.at[k, c], ar_out.at[k, 8], ar_sem.at[k, 8], at_c)

    def settle(k):
        landed(final.at[k, 1 - c], ar_sem.at[k, 8])

    begin(0)
    load_zeta.wait()
    for n in range(len(pieces)):
        pass_on(n)
        begin(n + 1)
        joined(n)
        term(n)
    forward(1)
    pass_on(5)
    forward(2)
    joined(5)
    for k in range(kpts):
        own_term(k)
    load_orb.wait()
    for k in range(3):
        arrived(k)
        combine(k)
    for k in range(3):
        scatter_y(k)
    for k in range(3):
        swap_z(k)
    arrived(3)
    combine(3)
    scatter_y(3)
    for k in range(3):
        gather_y(k)
    swap_z(3)
    gather_y(3)
    for k in range(kpts):
        gather_c(k)
    for k in range(kpts):
        settle(k)
    for copy in sent:
        copy.wait_send()


def exchange(zeta, coefs, orbitals, pair_table, counts):
    rows, points = zeta.shape
    kpts, _, share, bands = coefs.shape
    tile = min(TILE, rows)
    slice_ = bands // (NC * NY)
    f32, bf16, i16 = jnp.float32, jnp.bfloat16, jnp.int16
    hbm = pl.BlockSpec(memory_space=pltpu.HBM)
    smem = pl.BlockSpec(memory_space=pltpu.SMEM)
    vmem = pl.BlockSpec(memory_space=pltpu.VMEM)
    dma = pltpu.SemaphoreType.DMA
    most = rows * max(max(RELAY), 1) // RELAY_UNIT
    shapes = ((kpts, rows, bands), (kpts, NC, NY, slice_, bands))
    return pl.pallas_call(
        kernel,
        out_shape=tuple(pltpu.VMEM(shape, f32) for shape in shapes),
        in_specs=[smem, smem, hbm, hbm, hbm],
        out_specs=(vmem, vmem),
        scratch_shapes=[
            pltpu.VMEM((rows, points), bf16),
            pltpu.VMEM((kpts, 2, share, bands), bf16),
            pltpu.VMEM((2 * kpts, share, bands), bf16),
            pltpu.VMEM((2 * kpts, NZ, NY, NC, share, bands), bf16),
            pltpu.VMEM((kpts, rows, bands), bf16),
            pltpu.VMEM((kpts, rows, bands), i16),
            pltpu.VMEM((kpts, rows, bands), i16),
            pltpu.VMEM((kpts, most, bands), i16),
            pltpu.VMEM((kpts, rows // tile, 1, bands), f32),
            pltpu.VMEM((kpts, rows // tile, 1, bands), f32),
            pltpu.VMEM((kpts, NC, NY, slice_, bands), f32),
            pltpu.VMEM((kpts, NY, slice_, bands), f32),
            pltpu.VMEM((kpts, NY, slice_, bands), f32),
            pltpu.VMEM((kpts, NY - 1, slice_, bands), f32),
            pltpu.VMEM((kpts, slice_, bands), f32),
            pltpu.VMEM((kpts, slice_, bands), f32),
            dma((3,)),
            dma((kpts + 1, NZ)),
            dma((kpts + 1, NZ)),
            dma((2,)),
            dma((kpts + 2, 7)),
            dma((kpts + 2, 7)),
            dma((kpts + 1, 2)),
            dma((kpts + 1, 2)),
            dma((kpts, 2)),
            dma((kpts, 2)),
            dma((kpts, 9)),
            dma((kpts, 9)),
        ],
        compiler_params=pltpu.CompilerParams(collective_id=0, has_side_effects=True, vmem_limit_bytes=61_700_000),
        name="exchange",
    )(pair_table.T, counts, zeta, coefs, orbitals)


def on_device(zeta_sets, coef_blocks, pair_table, band_counts, orbitals):
    fields, intersection = exchange(zeta_sets[0], coef_blocks, orbitals, pair_table, band_counts)
    kpts, bands = fields.shape[0], fields.shape[2]
    return fields, intersection.reshape(kpts, bands, bands)


def solution(mesh):
    return jax.shard_map(
        on_device,
        mesh=mesh,
        in_specs=(
            P("blk", "slab", None),
            P("blk", None, "slab", None),
            P("blk", None),
            P("blk"),
            P("blk", "slab", None),
        ),
        out_specs=(P("blk", "slab", None), P("blk", None, None)),
        check_vma=False,
    )
```

time: 199 us -> 130 us (0.65)
  Pallas kernels: 188 us -> 127 us
  other arithmetic: 5.79 us -> 0 us
    pallas_call x1, Pallas kernels: 188 us -> 127 us  [exchange(): pl.pallas_call(kernel, out_shape=tuple((pltpu.VMEM(shape, f32) for shape...]
    select_n x2 -> x0, other arithmetic: 3.54 us -> none  [the longest x1 2.4 us: on_device(): jnp.where(keep[:, :, None], intersection, jnp.zeros((), jnp.float32))]
    unnamed x1 -> x2, local copies, waits for them, and re-layouts: 4.57 us -> 2.99 us
where the time goes in v2:
time: 130 us
  Pallas kernels  127 us (98%)
  local copies, waits for them, and re-layouts  2.99 us (2%)
    pallas_call x1, Pallas kernels, exchange(): pl.pallas_call(kernel, out_shape=tuple((pltpu.VMEM(shape, f32) for shape...  127 us
    unnamed x2, local copies, waits for them, and re-layouts  2.99 us

profile of v2, /device:TPU:1, one launch (start us, length us, event | category | flops | bytes accessed | tf_op | source)
XLA Modules:
  0.0 130.2 jit_solution(7404984967044870480)
XLA Ops:
  0.6 126.6 %exchange.1 = (f32[4,1024,256]{2,1,0:T(8,128)S(1)}, f32[4,2,4,32,256]{4,3,2,1,0:T(8,128)S(1)}) custom-call(s32[2,4]{1,0:T(2,128)} %bitcast.5, s32[4]{0:T(128)} %counts.1, bf16[1024,2048]{1,0:T(8,128)(2,1)} %bitcast.4, bf16[4,2,128,256]{3,2,1,0:T(8,128)(2,1)} %coef_in.1, bf16[4,1024,256]{2,1,0:T(8,128)(2,1)} %orb_in.1), custom_call_target="tpu_custom_call" | custom-call | tf_op jit(solution)/shard_map/exchange/pallas_call | solution.py:292
  127.2 2.0 %copy.9 = f32[4,1024,256]{2,1,0:T(8,128)} copy(f32[4,1024,256]{2,1,0:T(8,128)S(1)} %get-tuple-element.6) | data formatting | bytes 8388608
  129.2 1.0 copy.10

commit v3 on v2

--- a/solution.py
+++ b/solution.py
@@ -94,16 +94,19 @@
     pl.semaphore_wait(barrier, len(greeted))
 
     wide, narrow = pl.ds(0, bands), bands // 2
-    pieces = [(0, pl.ds(0, narrow)), (0, pl.ds(narrow, narrow))] + [(k, wide) for k in range(1, kpts)]
+    halves = (pl.ds(0, narrow), pl.ds(narrow, narrow))
+    last = kpts - 1
+    pieces = [(0, cols) for cols in halves] + [(k, wide) for k in range(1, last)] + [(last, cols) for cols in halves]
+    units = [(k, wide) for k in range(last)] + [(last, cols) for cols in halves]
     for n, (k, cols) in enumerate(pieces):
         for zz in range(NZ):
             send(picked.at[k, :, cols], coef.at[k, z, y, c, :, cols], pair_out.at[n, zz], pair_sem.at[n, z], near(before, zz))
-    nearest = pl.ds(kpts, kpts)
+    nearest, pack = pl.ds(kpts, kpts), kpts // 2
     send(picked.at[nearest], coef.at[nearest, z, y, c], cz_sem.at[1], cz_sem.at[0], at_z)
 
     def view(n, at, cc):
-        if n == len(pieces):
-            return coef.at[nearest, :, at, cc]
+        if n >= len(pieces):
+            return coef.at[pl.ds(kpts + (n - len(pieces)) * pack, pack), :, at, cc]
         return coef.at[pieces[n][0], :, at, cc, :, pieces[n][1]]
 
     def spread(n):
@@ -127,7 +130,7 @@
     def begin(n):
         if n == len(pieces):
             landed(coef.at[nearest, 1 - z, y, c], cz_sem.at[0])
-        else:
+        elif n < len(pieces):
             moved(n)
         spread(n)
 
@@ -153,12 +156,18 @@
             ssend[k, r, :, cols] = top / LEVELS
             return carry
 
-        lax.fori_loop(0, tiles, step, 0)
         direct, other = parts(k)
-        if extra(k):
-            send(psend.at[k, other], middle.at[k, pl.ds(0, extra(k))], relay_out.at[k, 0], relay_sem.at[k, 0], relay_to)
+        if n == 0:
+            for side in range(2):
+                lax.fori_loop(side * tiles // 2, (side + 1) * tiles // 2, step, 0)
+                some = pl.ds(side * rows // 2, rows // 2)
+                send(psend.at[k, some, cols], precv.at[k, some, cols], p_out.at[n, 2 * side], p_sem.at[n, 2 * side], at_after)
+        else:
+            lax.fori_loop(0, tiles, step, 0)
+            if extra(k):
+                send(psend.at[k, other], middle.at[k, pl.ds(0, extra(k))], relay_out.at[k, 0], relay_sem.at[k, 0], relay_to)
+            send(psend.at[k, direct, cols], precv.at[k, direct, cols], p_out.at[n, 0], p_sem.at[n, 0], at_after)
         send(ssend.at[k, :, :, cols], srecv.at[k, :, :, cols], p_out.at[n, 1], p_sem.at[n, 1], at_after)
-        send(psend.at[k, direct, cols], precv.at[k, direct, cols], p_out.at[n, 0], p_sem.at[n, 0], at_after)
 
     def forward(k):
         if extra(k):
@@ -173,73 +182,87 @@
 
         lax.fori_loop(0, tiles, step, 0)
 
-    def arrived(k):
+    def arrived(u):
+        k, wanted = units[u]
         direct, other = parts(k)
         for n, (owner, cols) in enumerate(pieces):
-            if owner == k:
+            if owner != k or wanted not in (wide, cols):
+                continue
+            if n == 0:
+                for side in range(2):
+                    landed(precv.at[k, pl.ds(side * rows // 2, rows // 2), cols], p_sem.at[n, 2 * side])
+            else:
                 landed(precv.at[k, direct, cols], p_sem.at[n, 0])
-                landed(srecv.at[k, :, :, cols], p_sem.at[n, 1])
+            landed(srecv.at[k, :, :, cols], p_sem.at[n, 1])
         if extra(k):
             landed(precv.at[k, other], relay_sem.at[k, 1])
 
-    def combine(k):
-        keep = lax.broadcasted_iota(jnp.int32, (1, bands), 1) < counts[k]
-        weight = jnp.where(keep, 1.0, 0.0)
-        weight_low = weight.astype(jnp.bfloat16)
+    def combine(u):
+        k, cols = units[u]
+        lane = lax.broadcasted_iota(jnp.int32, (1, bands), 1)
+        weight = jnp.where(lane[:, : cols.size] + cols.start < counts[k], 1.0, 0.0)
+        weight_low = jnp.where(lane < counts[k], 1.0, 0.0).astype(jnp.bfloat16)
 
         def step(r, carry):
             at = pl.ds(pl.multiple_of(r * tile, tile), tile)
-            value = field[k, at, :] + precv[k, at, :].astype(jnp.int32).astype(jnp.float32) * srecv[k, r]
-            value = value * weight
-            field[k, at, :] = value
+            level = precv[k, at, cols].astype(jnp.int32).astype(jnp.float32)
+            value = (field[k, at, cols] + level * srecv[k, r, :, cols]) * weight
+            field[k, at, cols] = value
             high = value.astype(jnp.bfloat16)
             low = (value - high.astype(jnp.float32)).astype(jnp.bfloat16)
             lines = orb[k, at, :] * weight_low
             over = (((0,), (0,)), ((), ()))
             added = lax.dot_general(lines, high, over, preferred_element_type=jnp.float32)
             added += lax.dot_general(lines, low, over, preferred_element_type=jnp.float32)
-            added = added.reshape(part.shape[1:])
+            added = added.reshape(*part.shape[1:4], cols.size)
 
             @pl.when(r == 0)
             def _():
-                part[k] = added
+                part[k, :, :, :, cols] = added
 
             @pl.when(r > 0)
             def _():
-                part[k] += added
+                part[k, :, :, :, cols] += added
 
             return carry
 
         lax.fori_loop(0, tiles, step, 0)
-        send(part.at[k, 1 - c], rsib.at[k], ar_out.at[k, 0], ar_sem.at[k, 0], at_c)
-
-    def scatter_y(k):
-        landed(rsib.at[k], ar_sem.at[k, 0])
-        half[k] = part[k, c] + rsib[k]
+        send(part.at[k, 1 - c, :, :, cols], rsib.at[k, :, :, cols], ar_out.at[u, 0], ar_sem.at[u, 0], at_c)
+
+    def scatter_y(u):
+        k, cols = units[u]
+        landed(rsib.at[k, :, :, cols], ar_sem.at[u, 0])
+        half[k, :, :, cols] = part[k, c, :, :, cols] + rsib[k, :, :, cols]
         for d in range(1, NY):
-            send(half.at[k, ys[d]], ry.at[k, d - 1], ar_out.at[k, d], ar_sem.at[k, d], at_y[d])
-
-    def swap_z(k):
-        total = half[k, y]
+            send(half.at[k, ys[d], :, cols], ry.at[k, d - 1, :, cols], ar_out.at[u, d], ar_sem.at[u, d], at_y[d])
+
+    def swap_z(u):
+        k, cols = units[u]
+        total = half[k, y, :, cols]
         for d in range(1, NY):
-            landed(ry.at[k, d - 1], ar_sem.at[k, d])
-            total = total + ry[k, d - 1]
-        quarter[k] = total
-        send(quarter.at[k], rz.at[k], ar_out.at[k, 4], ar_sem.at[k, 4], at_z)
-
-    def gather_y(k):
-        landed(rz.at[k], ar_sem.at[k, 4])
-        final[k, c, y] = quarter[k] + rz[k]
+            landed(ry.at[k, d - 1, :, cols], ar_sem.at[u, d])
+            total = total + ry[k, d - 1, :, cols]
+        quarter[k, :, cols] = total
+        send(quarter.at[k, :, cols], rz.at[k, :, cols], ar_out.at[u, 4], ar_sem.at[u, 4], at_z)
+
+    def gather_y(u):
+        k, cols = units[u]
+        landed(rz.at[k, :, cols], ar_sem.at[u, 4])
+        final[k, c, y, :, cols] = quarter[k, :, cols] + rz[k, :, cols]
+        done = final.at[k, c, y, :, cols]
         for d in range(1, NY):
-            send(final.at[k, c, y], final.at[k, c, y], ar_out.at[k, 4 + d], ar_sem.at[k, 4 + d], at_y[d])
-
-    def gather_c(k):
+            send(done, done, ar_out.at[u, 4 + d], ar_sem.at[u, 4 + d], at_y[d])
+
+    def gather_c(u):
+        k, cols = units[u]
         for d in range(1, NY):
-            landed(final.at[k, c, ys[NY - d]], ar_sem.at[k, 4 + d])
-        send(final.at[k, c], final.at[k, c], ar_out.at[k, 8], ar_sem.at[k, 8], at_c)
-
-    def settle(k):
-        landed(final.at[k, 1 - c], ar_sem.at[k, 8])
+            landed(final.at[k, c, ys[NY - d], :, cols], ar_sem.at[u, 4 + d])
+        done = final.at[k, c, :, :, cols]
+        send(done, done, ar_out.at[u, 8], ar_sem.at[u, 8], at_c)
+
+    def settle(u):
+        k, cols = units[u]
+        landed(final.at[k, 1 - c, :, :, cols], ar_sem.at[u, 8])
 
     begin(0)
     load_zeta.wait()
@@ -248,31 +271,45 @@
         begin(n + 1)
         joined(n)
         term(n)
+    begin(7)
     forward(1)
-    pass_on(5)
+    pass_on(6)
     forward(2)
-    joined(5)
-    for k in range(kpts):
-        own_term(k)
+    joined(6)
+    own_term(0)
+    own_term(1)
     load_orb.wait()
-    for k in range(3):
-        arrived(k)
-        combine(k)
-    for k in range(3):
-        scatter_y(k)
-    for k in range(3):
-        swap_z(k)
+    arrived(0)
+    combine(0)
+    pass_on(7)
+    scatter_y(0)
+    joined(7)
+    own_term(2)
+    arrived(1)
+    combine(1)
+    swap_z(0)
+    own_term(3)
+    scatter_y(1)
+    arrived(2)
+    combine(2)
+    swap_z(1)
+    scatter_y(2)
     arrived(3)
     combine(3)
+    swap_z(2)
     scatter_y(3)
-    for k in range(3):
-        gather_y(k)
+    arrived(4)
+    combine(4)
     swap_z(3)
-    gather_y(3)
-    for k in range(kpts):
-        gather_c(k)
-    for k in range(kpts):
-        settle(k)
+    scatter_y(4)
+    for u in range(4):
+        gather_y(u)
+    swap_z(4)
+    gather_y(4)
+    for u in range(5):
+        gather_c(u)
+    for u in range(5):
+        settle(u)
     for copy in sent:
         copy.wait_send()
 
@@ -312,17 +349,17 @@
             pltpu.VMEM((kpts, slice_, bands), f32),
             pltpu.VMEM((kpts, slice_, bands), f32),
             dma((3,)),
-            dma((kpts + 1, NZ)),
-            dma((kpts + 1, NZ)),
+            dma((kpts + 2, NZ)),
+            dma((kpts + 2, NZ)),
             dma((2,)),
-            dma((kpts + 2, 7)),
-            dma((kpts + 2, 7)),
-            dma((kpts + 1, 2)),
-            dma((kpts + 1, 2)),
+            dma((kpts + 4, 7)),
+            dma((kpts + 4, 7)),
+            dma((kpts + 2, 3)),
+            dma((kpts + 2, 3)),
             dma((kpts, 2)),
             dma((kpts, 2)),
-            dma((kpts, 9)),
-            dma((kpts, 9)),
+            dma((kpts + 1, 9)),
+            dma((kpts + 1, 9)),
         ],
         compiler_params=pltpu.CompilerParams(collective_id=0, has_side_effects=True, vmem_limit_bytes=61_700_000),
         name="exchange",

time: 130 us -> 124 us (0.954)
  Pallas kernels: 127 us -> 121 us
    pallas_call x1, Pallas kernels: 127 us -> 121 us  [exchange(): pl.pallas_call(kernel, out_shape=tuple((pltpu.VMEM(shape, f32) for shape...]
where the time goes in v3:
time: 124 us
  Pallas kernels  121 us (98%)
  local copies, waits for them, and re-layouts  2.99 us (2%)
    pallas_call x1, Pallas kernels, exchange(): pl.pallas_call(kernel, out_shape=tuple((pltpu.VMEM(shape, f32) for shape...  121 us
    unnamed x2, local copies, waits for them, and re-layouts  2.99 us

profile of v3, /device:TPU:1, one launch (start us, length us, event | category | flops | bytes accessed | tf_op | source)
XLA Modules:
  0.0 124.2 jit_solution(354480348481137657)
XLA Ops:
  0.6 120.6 %exchange.1 = (f32[4,1024,256]{2,1,0:T(8,128)S(1)}, f32[4,2,4,32,256]{4,3,2,1,0:T(8,128)S(1)}) custom-call(s32[2,4]{1,0:T(2,128)} %bitcast.5, s32[4]{0:T(128)} %counts.1, bf16[1024,2048]{1,0:T(8,128)(2,1)} %bitcast.4, bf16[4,2,128,256]{3,2,1,0:T(8,128)(2,1)} %coef_in.1, bf16[4,1024,256]{2,1,0:T(8,128)(2,1)} %orb_in.1), custom_call_target="tpu_custom_call" | custom-call | tf_op jit(solution)/shard_map/exchange/pallas_call | solution.py:329
  121.2 2.0 %copy.9 = f32[4,1024,256]{2,1,0:T(8,128)} copy(f32[4,1024,256]{2,1,0:T(8,128)S(1)} %get-tuple-element.6) | data formatting | bytes 8388608
  123.2 1.0 copy.10

commit v4 on v3

--- a/solution.py
+++ b/solution.py
@@ -20,8 +20,8 @@
 
 
 def kernel(
-    pair_table, counts, zeta_in, coef_in, orb_in, field, final,
-    zeta, raw, picked, coef, orb, psend, precv, middle, ssend, srecv,
+    table_in, counts_in, zeta_in, coef_in, orb_in, field, final,
+    pair_table, counts, zeta, raw, picked, coef, orb, psend, precv, middle, ssend, srecv,
     part, rsib, half, ry, quarter, rz,
     load_sem, pair_sem, pair_out, cz_sem, ag_sem, ag_out, p_sem, p_out, relay_sem, relay_out, ar_sem, ar_out,
 ):
@@ -72,6 +72,10 @@
     sent = []
     load_raw = pltpu.make_async_copy(coef_in, raw, load_sem.at[0])
     load_raw.start()
+    load_table = pltpu.make_async_copy(table_in, pair_table, load_sem.at[3])
+    load_table.start()
+    load_counts = pltpu.make_async_copy(counts_in, counts, load_sem.at[4])
+    load_counts.start()
     load_zeta = pltpu.make_async_copy(zeta_in, zeta, load_sem.at[1])
     load_zeta.start()
     load_orb = pltpu.make_async_copy(orb_in, orb, load_sem.at[2])
@@ -83,6 +87,8 @@
     ]
     for where in greeted:
         pl.semaphore_signal(barrier, inc=1, device_id=where, device_id_type=pl.DeviceIdType.MESH)
+    load_table.wait()
+    load_counts.wait()
     load_raw.wait()
     for k in range(kpts):
         swap = jnp.full(raw.shape[2:], pair_table[0, k], jnp.int32) == 1
@@ -321,7 +327,6 @@
     slice_ = bands // (NC * NY)
     f32, bf16, i16 = jnp.float32, jnp.bfloat16, jnp.int16
     hbm = pl.BlockSpec(memory_space=pltpu.HBM)
-    smem = pl.BlockSpec(memory_space=pltpu.SMEM)
     vmem = pl.BlockSpec(memory_space=pltpu.VMEM)
     dma = pltpu.SemaphoreType.DMA
     most = rows * max(max(RELAY), 1) // RELAY_UNIT
@@ -329,9 +334,11 @@
     return pl.pallas_call(
         kernel,
         out_shape=tuple(pltpu.VMEM(shape, f32) for shape in shapes),
-        in_specs=[smem, smem, hbm, hbm, hbm],
+        in_specs=[hbm, hbm, hbm, hbm, hbm],
         out_specs=(vmem, vmem),
         scratch_shapes=[
+            pltpu.SMEM((2, kpts), jnp.int32),
+            pltpu.SMEM((kpts,), jnp.int32),
             pltpu.VMEM((rows, points), bf16),
             pltpu.VMEM((kpts, 2, share, bands), bf16),
             pltpu.VMEM((2 * kpts, share, bands), bf16),
@@ -348,7 +355,7 @@
             pltpu.VMEM((kpts, NY - 1, slice_, bands), f32),
             pltpu.VMEM((kpts, slice_, bands), f32),
             pltpu.VMEM((kpts, slice_, bands), f32),
-            dma((3,)),
+            dma((5,)),
             dma((kpts + 2, NZ)),
             dma((kpts + 2, NZ)),
             dma((2,)),
@@ -361,7 +368,7 @@
             dma((kpts + 1, 9)),
             dma((kpts + 1, 9)),
         ],
-        compiler_params=pltpu.CompilerParams(collective_id=0, has_side_effects=True, vmem_limit_bytes=61_700_000),
+        compiler_params=pltpu.CompilerParams(collective_id=0, has_side_effects=True, vmem_limit_bytes=61_800_000),
         name="exchange",
     )(pair_table.T, counts, zeta, coefs, orbitals)
 

time: 124 us -> 124 us (level)
  no operation moved by 1% of the time
where the time goes in v4:
time: 124 us
  Pallas kernels  120 us (97%)
  local copies, waits for them, and re-layouts  2.99 us (2%)
    pallas_call x1, Pallas kernels, exchange(): pl.pallas_call(kernel, out_shape=tuple((pltpu.VMEM(shape, f32) for shape...  120 us
    unnamed x2, local copies, waits for them, and re-layouts  2.99 us

profile of v4, /device:TPU:1, one launch (start us, length us, event | category | flops | bytes accessed | tf_op | source)
XLA Modules:
  0.0 123.6 jit_solution(16961460164958896883)
XLA Ops:
  0.6 120.0 %exchange.1 = (f32[4,1024,256]{2,1,0:T(8,128)S(1)}, f32[4,2,4,32,256]{4,3,2,1,0:T(8,128)S(1)}) custom-call(s32[2,4]{1,0:T(2,128)} %bitcast.5, s32[4]{0:T(128)} %counts_in.1, bf16[1024,2048]{1,0:T(8,128)(2,1)} %bitcast.4, bf16[4,2,128,256]{3,2,1,0:T(8,128)(2,1)} %coef_in.1, bf16[4,1024,256]{2,1,0:T(8,128)(2,1)} %orb_in.1), custom_call_target="tpu_custom_call" | custom-call | tf_op jit(solution)/shard_map/exchange/pallas_call | solution.py:334
  120.6 2.0 %copy.9 = f32[4,1024,256]{2,1,0:T(8,128)} copy(f32[4,1024,256]{2,1,0:T(8,128)S(1)} %get-tuple-element.6) | data formatting | bytes 8388608
  122.6 1.0 copy.10
